TPU v7x, 32 devices: a whole 2x2x4 slice. The times are simulated.
32 devices in a mesh: dp: 8 (over y, x, core), mp: 4 (over z).
Axes of the slice: x: 2, y: 2, z: 4, core: 2. Of those that a mesh axis runs over, the one named last changes fastest.
Arguments:
- images: bfloat16 [1536, 1024], P('dp', 'mp'), may hold values from -80 to 80, as said below
- texts: bfloat16 [1536, 1024], P('dp', 'mp'), may hold values from -80 to 80, as said below
- logit_scale: float32 [1], replicated, may hold values from 240 to 300
Outputs:
- row_loss: float32 [1536], P('dp')
- column_loss: float32 [1536], P('dp')
Inputs may be any that keep to these rules, and one draw needn't show every extreme that they name: `images`: Real-valued entries. `texts`: Real-valued entries.
All inputs are finite; a program needn't handle non-finite values.
Results may differ from a plain program's by a relative error of at most 0.0044.
Values may be sent and summed in bfloat16 or wider, within the bound.
A program may use at most 64 MiB of HBM per device.

v0:
```python
import functools

import jax
import jax.numpy as jnp
from jax import lax
from jax.experimental import pallas as pl
from jax.experimental.pallas import tpu as pltpu
from jax.sharding import PartitionSpec as P

F32 = jnp.float32
MESH = pl.DeviceIdType.MESH
CORES = 2
CHUNKS = 2


def dot_t(a, b):
    return lax.dot_general(a, b, (((1,), (1,)), ((), ())), preferred_element_type=F32)


def unit_slices(slices):
    wide = [s.astype(F32) for s in slices]
    square = functools.reduce(lambda p, q: p + q, [w * w for w in wide])
    inv = lax.rsqrt(jnp.sum(square, axis=1, keepdims=True) + 1e-06)
    return [(w * inv).astype(jnp.bfloat16) for w in wide]


def top_total(scores):
    top = jnp.max(scores, axis=0, keepdims=True)
    return top, jnp.sum(jnp.exp(scores - top), axis=0, keepdims=True)


def loss_kernel(
    groups,
    slices,
    scale_ref,
    img_hbm,
    txt_hbm,
    out_ref,
    img,
    txt,
    txt_out,
    row_msg,
    col_msg,
    row_got,
    col_got,
    load_sem,
    word,
    tz_send,
    tx_send,
    txt_recv,
    ir_send,
    il_send,
    ip_send,
    iz_recv,
    ip_recv,
    row_send,
    row_recv,
    col_send,
    col_recv,
):
    dp = lax.axis_index("dp")
    m = lax.axis_index("mp")
    h = dp // CORES
    c = dp % CORES
    partner = dp + 1 - 2 * c
    quarter = txt.shape[2]
    rows = out_ref.shape[1]
    spare = col_msg.shape[2] // 2

    load_txt = pltpu.make_async_copy(txt_hbm, txt_out, load_sem.at[0])
    load_own = pltpu.make_async_copy(txt_hbm.at[m], txt.at[m, h], load_sem.at[1])
    load_img = pltpu.make_async_copy(img_hbm, img.at[c, m], load_sem.at[2])
    load_txt.start()
    load_own.start()
    load_img.start()

    barrier = pltpu.get_barrier_semaphore()

    def group_peer(k):
        return lax.rem(h + k, groups)

    def slice_peer(k):
        return lax.rem(m + k, slices)

    def greet(to_dp, to_mp):
        pl.semaphore_signal(
            barrier, inc=1, device_id={"dp": to_dp, "mp": to_mp}, device_id_type=MESH
        )

    has_left = m >= 1
    has_right = m + 1 < slices
    left = jnp.maximum(m - 1, 0)
    right = jnp.minimum(m + 1, slices - 1)
    pl.when(has_left)(lambda: greet(dp, left))
    pl.when(has_right)(lambda: greet(dp, right))
    greet(partner, m)
    for k in range(1, groups):
        greet(group_peer(k) * CORES + c, m)
    pl.semaphore_wait(barrier, groups + has_left.astype(jnp.int32) + has_right.astype(jnp.int32))

    def send(src, dst, s_sem, r_sem, to_dp, to_mp):
        return pltpu.make_async_remote_copy(
            src_ref=src,
            dst_ref=dst,
            send_sem=s_sem,
            recv_sem=r_sem,
            device_id={"dp": to_dp, "mp": to_mp},
            device_id_type=MESH,
        )

    pending = []

    def go(copy):
        copy.start()
        pending.append((None, copy))

    load_img.wait()

    def pass_on(b, q, right, left):
        block = img.at[c, b, q]
        if right is not None:
            r = send(block, block, ir_send.at[b, q], iz_recv.at[b, q], dp, jnp.minimum(m + 1, slices - 1))
            pl.when(right)(r.start)
            pending.append((right, r))
        if left is not None:
            l = send(block, block, il_send.at[b, q], iz_recv.at[b, q], dp, jnp.maximum(m - 1, 0))
            pl.when(left)(l.start)
            pending.append((left, l))

    def to_partner(b, q):
        block = img.at[c, b, q]
        return send(block, block, ip_send.at[b, q], ip_recv.at[b, q], partner, m)

    for q in range(CHUNKS):
        pass_on(m, q, m + 1 < slices, m >= 1)
    load_txt.wait()
    def tell(to, sem):
        pl.semaphore_signal(
            sem, inc=1, device_id={"dp": dp, "mp": to}, device_id_type=MESH
        )

    def text_to(to, cond):
        copy = send(txt_out.at[to], txt.at[m, h], tz_send.at[to], txt_recv.at[m, h], dp, to)
        pl.when(cond)(copy.start)
        pending.append((cond, copy))

    for d in range(1, slices):
        if d > 1:
            pl.when(has_right & (m - (d - 1) >= 0))(lambda: tell(right, word.at[0]))
            pl.when(has_left & (m + (d - 1) < slices))(lambda: tell(left, word.at[1]))
            pl.when(m - d >= 0)(lambda: pl.semaphore_wait(word.at[0], 1))
            pl.when(m + d < slices)(lambda: pl.semaphore_wait(word.at[1], 1))
        text_to(jnp.maximum(m - d, 0), m - d >= 0)
        text_to(jnp.minimum(m + d, slices - 1), m + d < slices)

    def spread(s):
        for k in reversed(range(1, groups)):
            to = group_peer(k) * CORES + c
            go(send(txt.at[s, h], txt.at[s, h], tx_send.at[s, k], txt_recv.at[s, h], to, m))

    load_own.wait()
    spread(m)

    for q in range(CHUNKS):
        go(to_partner(m, q))

    def landed(ref, sem):
        pltpu.make_async_copy(ref, ref, sem).wait()

    def texts_in(k):
        s = slice_peer(k)
        landed(txt.at[s, h], txt_recv.at[s, h])
        spread(s)

    for k in range(1, slices):
        for q in range(CHUNKS):
            low = m - k
            high = m + k
            has_low = low >= 0
            has_high = high < slices
            low_i = jnp.maximum(low, 0)
            high_i = jnp.minimum(high, slices - 1)

            def take(b):
                landed(img.at[c, b, q], iz_recv.at[b, q])

            pl.when(has_low)(functools.partial(take, low_i))
            pass_on(low_i, q, jnp.logical_and(has_low, m + 1 < slices), None)
            pl.when(has_high)(functools.partial(take, high_i))
            pass_on(high_i, q, None, jnp.logical_and(has_high, m >= 1))
            low_p = to_partner(low_i, q)
            pl.when(has_low)(low_p.start)
            pending.append((has_low, low_p))
            high_p = to_partner(high_i, q)
            pl.when(has_high)(high_p.start)
            pending.append((has_high, high_p))

            if k == 1 and q == CHUNKS - 1:
                for j in range(1, slices):
                    texts_in(j)

    for k in range(1, groups):
        for s in range(slices):
            landed(txt.at[s, group_peer(k)], txt_recv.at[s, group_peer(k)])

    scale = scale_ref[0]
    width = txt.shape[3]
    text_unit = unit_slices([txt[s].reshape(groups * quarter, width) for s in range(slices)])

    def tile(which, own):
        unit = unit_slices([img[which, s].reshape(rows, width) for s in range(slices)])
        by_row = scale * functools.reduce(
            lambda p, q: p + q, [dot_t(t, u) for t, u in zip(text_unit, unit)]
        )
        by_col = scale * functools.reduce(
            lambda p, q: p + q, [dot_t(u, t) for t, u in zip(text_unit, unit)]
        )
        row_top, row_total = top_total(by_row)
        message = jnp.concatenate([row_top, row_total], axis=0)
        row_msg[which] = message
        for k in range(1 if own else 0, slices):
            to = slice_peer(k)
            go(
                send(
                    row_msg.at[which],
                    row_got.at[c, m],
                    row_send.at[which, k],
                    row_recv.at[c, m],
                    dp if own else partner,
                    to,
                )
            )
        if own:
            row_got[c, m] = message
            image_row = lax.broadcasted_iota(jnp.int32, by_col.shape, 0) - m * quarter
            text_row = lax.broadcasted_iota(jnp.int32, by_col.shape, 1) - h * quarter
            pair = (text_row == image_row) & (text_row >= 0) & (text_row < quarter)
            matched = jnp.sum(jnp.where(pair, by_col, 0.0), axis=0, keepdims=True)
            return top_total(by_col) + (matched,)
        return top_total(by_col)

    top_a, total_a, own_matched = tile(c, True)
    for s in range(slices):
        for q in range(CHUNKS):
            landed(img.at[1 - c, s, q], ip_recv.at[s, q])
    top_b, total_b = tile(1 - c, False)
    col_top = jnp.maximum(top_a, top_b)
    col_total = total_a * jnp.exp(top_a - col_top) + total_b * jnp.exp(top_b - col_top)
    for g in range(groups):
        part = slice(g * quarter, (g + 1) * quarter)
        col_msg[g, 0:2, 0:quarter] = jnp.concatenate([col_top[:, part], col_total[:, part]], axis=0)
        col_msg[g, 0:1, spare : spare + quarter] = own_matched[:, part]
    col_got[m, h] = col_msg[h]
    for k in reversed(range(groups)):
        g = group_peer(k)
        for j in range(slices):
            if k == 0 and j == 0:
                continue
            go(
                send(
                    col_msg.at[g],
                    col_got.at[m, h],
                    col_send.at[k, j],
                    col_recv.at[m, h],
                    g * CORES + c,
                    slice_peer(j),
                )
            )

    for k in range(slices):
        s = slice_peer(k)
        if k > 0:
            landed(row_got.at[c, s], row_recv.at[c, s])
        landed(row_got.at[1 - c, s], row_recv.at[1 - c, s])
    got = row_got[...].reshape(CORES * slices, *row_got.shape[2:])
    peak = jnp.max(got[:, 0, :], axis=0, keepdims=True)
    whole = jnp.sum(got[:, 1, :] * jnp.exp(got[:, 0, :] - peak), axis=0, keepdims=True)
    row_lse = peak + jnp.log(whole)

    for k in range(groups):
        g = group_peer(k)
        for j in range(slices):
            if k == 0 and j == 0:
                continue
            s = slice_peer(j)
            landed(col_got.at[s, g], col_recv.at[s, g])
    pieces = []
    pairs = []
    for s in range(slices):
        tops = col_got[s, :, 0, 0:quarter]
        totals = col_got[s, :, 1, 0:quarter]
        peak = jnp.max(tops, axis=0, keepdims=True)
        pieces.append(
            peak + jnp.log(jnp.sum(totals * jnp.exp(tops - peak), axis=0, keepdims=True))
        )
        pairs.append(jnp.sum(col_got[s, :, 0, spare : spare + quarter], axis=0, keepdims=True))
    matched = jnp.concatenate(pairs, axis=1)
    out_ref[...] = jnp.concatenate([row_lse, jnp.concatenate(pieces, axis=1)], axis=0) - matched

    for cond, copy in pending:
        if cond is None:
            copy.wait_send()
        else:
            pl.when(cond)(copy.wait_send)


def kernel_on_device(groups, slices, images, texts, logit_scale):
    rows, width = images.shape
    quarter = rows // slices
    lanes = 128 * pl.cdiv(2 * quarter, 128)
    dma = pltpu.SemaphoreType.DMA
    vmem = pl.BlockSpec(memory_space=pltpu.VMEM)
    hbm = pl.BlockSpec(memory_space=pl.ANY)
    losses = pl.pallas_call(
        functools.partial(loss_kernel, groups, slices),
        out_shape=jax.ShapeDtypeStruct((2, rows), F32),
        in_specs=[pl.BlockSpec(memory_space=pltpu.SMEM), hbm, hbm],
        out_specs=vmem,
        scratch_shapes=[
            pltpu.VMEM((CORES, slices, CHUNKS, rows // CHUNKS, width), images.dtype),
            pltpu.VMEM((slices, groups, quarter, width), texts.dtype),
            pltpu.VMEM((slices, quarter, width), texts.dtype),
            pltpu.VMEM((CORES, 2, rows), F32),
            pltpu.VMEM((groups, 2, lanes), F32),
            pltpu.VMEM((CORES, slices, 2, rows), F32),
            pltpu.VMEM((slices, groups, 2, lanes), F32),
            dma((3,)),
            pltpu.SemaphoreType.REGULAR((2,)),
            dma((slices,)),
            dma((slices, groups)),
            dma((slices, groups)),
            dma((slices, CHUNKS)),
            dma((slices, CHUNKS)),
            dma((slices, CHUNKS)),
            dma((slices, CHUNKS)),
            dma((slices, CHUNKS)),
            dma((CORES, slices)),
            dma((CORES, slices)),
            dma((groups, slices)),
            dma((slices, groups)),
        ],
        compiler_params=pltpu.CompilerParams(collective_id=0, has_side_effects=True),
    )(
        logit_scale,
        images.reshape(CHUNKS, rows // CHUNKS, width),
        texts.reshape(slices, quarter, width),
    )
    return losses[0], losses[1]


def normalize(rows):
    values = rows.astype(F32)
    return (values * lax.rsqrt(jnp.sum(values * values, axis=1, keepdims=True) + 1e-06)).astype(
        jnp.bfloat16
    )


def collectives_on_device(images, texts, logit_scale):
    count = lax.axis_size("dp")
    m = lax.axis_index("mp")
    image_unit = normalize(lax.all_gather(images, "mp", axis=1, tiled=True))
    text_unit = normalize(lax.all_to_all(texts, "mp", split_axis=0, concat_axis=1, tiled=True))
    scale = logit_scale[0]
    quarter = text_unit.shape[0]
    mine = lax.dynamic_slice_in_dim(image_unit, m * quarter, quarter, 0)
    matched = scale * jnp.sum(mine.astype(F32) * text_unit.astype(F32), axis=1)
    scores = scale * dot_t(lax.all_gather(text_unit, "dp", axis=0, tiled=True), image_unit)
    row_top = jnp.max(scores, axis=0)
    row_total = jnp.sum(jnp.exp(scores - row_top[None, :]), axis=0)
    col_top = jnp.max(scores, axis=1)
    col_total = jnp.sum(jnp.exp(scores - col_top[:, None]), axis=1)
    got_top, got_total = (
        lax.all_to_all(v.reshape(count, quarter), "dp", split_axis=0, concat_axis=0, tiled=True)
        for v in (col_top, col_total)
    )
    col_peak = jnp.max(got_top, axis=0)
    col_lse = col_peak + jnp.log(jnp.sum(got_total * jnp.exp(got_top - col_peak[None, :]), axis=0))
    row_peak = lax.pmax(row_top, "mp")
    row_lse = row_peak + jnp.log(lax.psum(row_total * jnp.exp(row_top - row_peak), "mp"))
    col_full = lax.all_gather(col_lse, "mp", axis=0, tiled=True)
    matched_full = lax.all_gather(matched, "mp", axis=0, tiled=True)
    return row_lse - matched_full, col_full - matched_full


def solution(mesh):
    dp, mp = mesh.shape["dp"], mesh.shape["mp"]
    small = dp % CORES == 0 and dp * mp <= 64
    body = (
        functools.partial(kernel_on_device, dp // CORES, mp) if small else collectives_on_device
    )
    return jax.shard_map(
        body,
        mesh=mesh,
        in_specs=(P("dp", "mp"), P("dp", "mp"), P()),
        out_specs=(P("dp"), P("dp")),
        check_vma=False,
    )
```

profile of v0, /device:TPU:0, one launch (start us, length us, event | category | flops | bytes accessed | tf_op | source)
XLA Modules:
  0.0 25.8 jit_solution(13727838701298688248)
XLA Ops:
  1.3 23.2 %shard_map.50 = f32[2,192]{1,0:T(2,128)} custom-call(f32[1]{0:T(128)S(6)} %copy.5.scale_ref, bf16[2,96,256]{2,1,0:T(8,128)(2,1)} %bitcast.4, bf16[4,48,256]{2,1,0:T(8,128)(2,1)} %bitcast.5), custom_call_target="tpu_custom_call" | custom-call | tf_op jit(solution)/shard_map/pallas_call | solution.py:314
  24.5 1.3 %fusion = (f32[1,192]{1,0:T(1,128)}, f32[1,192]{1,0:T(1,128)}) fusion(f32[2,192]{1,0:T(2,128)} %shard_map.50), kind=kLoop, calls=%fused_computation | loop fusion | bytes 3072 | tf_op jit(solution)/shard_map/slice | solution.py:348
where the time goes:
time: 26 us; the launch traced here: 25.8 us
  Pallas kernels  23.2 us (89%)
  local copies, waits for them, and re-layouts  1.32 us (5%)
  between operations  1.28 us (5%)
    pallas_call x1, Pallas kernels, kernel_on_device(): pl.pallas_call(functools.partial(loss_kernel, groups, slices), out_shape=...  23.2 us
    slice x1, local copies, waits for them, and re-layouts, kernel_on_device(): return (losses[0], losses[1])  1.32 us

commit v1 on v0

--- a/solution.py
+++ b/solution.py
@@ -313,7 +313,7 @@
     hbm = pl.BlockSpec(memory_space=pl.ANY)
     losses = pl.pallas_call(
         functools.partial(loss_kernel, groups, slices),
-        out_shape=jax.ShapeDtypeStruct((2, rows), F32),
+        out_shape=pltpu.VMEM((2, rows), F32),
         in_specs=[pl.BlockSpec(memory_space=pltpu.SMEM), hbm, hbm],
         out_specs=vmem,
         scratch_shapes=[

time: 26 us -> 24.7 us (0.950)
  local copies, waits for them, and re-layouts: 1.32 us -> 0.57 us
  Pallas kernels: 23.2 us -> 22.6 us
    slice x1, local copies, waits for them, and re-layouts: 1.32 us -> 0.57 us  [kernel_on_device(): return (losses[0], losses[1])]
    pallas_call x1, Pallas kernels: 23.2 us -> 22.6 us  [kernel_on_device(): pl.pallas_call(functools.partial(loss_kernel, groups, slices), out_shape=...]
where the time goes in v1:
time: 24.7 us; the launch traced here: 24.5 us
  Pallas kernels  22.6 us (91%)
  between operations  1.28 us (5%)
  local copies, waits for them, and re-layouts  0.57 us (2%)
    pallas_call x1, Pallas kernels, kernel_on_device(): pl.pallas_call(functools.partial(loss_kernel, groups, slices), out_shape=...  22.6 us
    slice x1, local copies, waits for them, and re-layouts, kernel_on_device(): return (losses[0], losses[1])  0.57 us

profile of v1, /device:TPU:0, one launch (start us, length us, event | category | flops | bytes accessed | tf_op | source)
XLA Modules:
  0.0 24.5 jit_solution(12452071382216721937)
XLA Ops:
  1.3 22.6 %shard_map.50 = f32[2,192]{1,0:T(2,128)S(1)} custom-call(f32[1]{0:T(128)S(6)} %copy.5.scale_ref, bf16[2,96,256]{2,1,0:T(8,128)(2,1)} %bitcast.4, bf16[4,48,256]{2,1,0:T(8,128)(2,1)} %bitcast.5), custom_call_target="tpu_custom_call" | custom-call | tf_op jit(solution)/shard_map/pallas_call | solution.py:314
  23.9 0.6 %fusion = (f32[1,192]{1,0:T(1,128)}, f32[1,192]{1,0:T(1,128)}) fusion(f32[2,192]{1,0:T(2,128)S(1)} %shard_map.50), kind=kLoop, calls=%fused_computation | loop fusion | bytes 3072 | tf_op jit(solution)/shard_map/slice | solution.py:348

commit v2 on v1

v2 whole, which is shorter than its diff:
```python
import functools

import jax
import jax.numpy as jnp
from jax import lax
from jax.experimental import pallas as pl
from jax.experimental.pallas import tpu as pltpu
from jax.sharding import PartitionSpec as P

F32 = jnp.float32
MESH = pl.DeviceIdType.MESH
CORES = 2
PLANE = 4
DEPTH = 4
CHUNKS = 2
OWN, NEAR, OTHER, FAR = range(4)
ACROSS_Z, ACROSS_X, ACROSS_Y, ACROSS_CORE, BEYOND = range(5)


def dot_t(a, b):
    return lax.dot_general(a, b, (((1,), (1,)), ((), ())), preferred_element_type=F32)


def top_total(scores):
    top = jnp.max(scores, axis=0, keepdims=True)
    return top, jnp.sum(jnp.exp(scores - top), axis=0, keepdims=True)


def squares(block):
    wide = block.astype(F32)
    square = wide * wide
    high = square.astype(jnp.bfloat16)
    low = (square - high.astype(F32)).astype(jnp.bfloat16)
    ones = jnp.ones((8, block.shape[1]), jnp.bfloat16)
    return dot_t(ones, high) + dot_t(ones, low), jnp.sum(square, axis=1, keepdims=True)


def loss_kernel(
    scale_ref,
    img_hbm,
    txt_hbm,
    out_ref,
    img,
    spare,
    txt,
    by_row,
    by_col,
    img_lane,
    txt_lane,
    img_sub,
    txt_sub,
    row_msg,
    col_msg,
    row_got,
    col_got,
    row_tally,
    col_tally,
    load_sem,
    img_recv,
    txt_recv,
    pair_recv,
    row_recv,
    col_recv,
    word,
    xy_send,
    pair_send,
    text_send,
    spare_send,
    row_send,
    col_send,
):
    dp = lax.axis_index("dp")
    m = lax.axis_index("mp")
    h = dp // CORES
    c = dp % CORES
    x = h % 2
    y = h // 2
    partner = dp + 1 - 2 * c
    beside = dp + CORES * (1 - 2 * x)
    above = dp + 2 * CORES * (1 - 2 * y)
    across = above + CORES * (1 - 2 * x)
    half = img.shape[2]
    rows = 2 * half

    low = DEPTH // 2 - 1
    inner = (m == low) | (m == low + 1)
    last = DEPTH - 1
    a = jnp.clip(m - low, 0, 1)
    other = last - m
    near = low + a
    far = last - near

    def signal(sem, to_dp, to_mp):
        pl.semaphore_signal(
            sem, inc=1, device_id={"dp": to_dp, "mp": to_mp}, device_id_type=MESH
        )

    def send(src, dst, s_sem, r_sem, to_dp, to_mp):
        pltpu.make_async_remote_copy(
            src_ref=src,
            dst_ref=dst,
            send_sem=s_sem,
            recv_sem=r_sem,
            device_id={"dp": to_dp, "mp": to_mp},
            device_id_type=MESH,
        ).start()

    def landed(ref, sem):
        pltpu.make_async_copy(ref, ref, sem).wait()

    load_text = pltpu.make_async_copy(txt_hbm, txt.at[OWN, 0], load_sem.at[0])
    load_spare = pltpu.make_async_copy(img_hbm, spare, load_sem.at[1])
    load_own = pltpu.make_async_copy(img_hbm.at[a], img.at[OWN, 0], load_sem.at[2])

    barrier = pltpu.get_barrier_semaphore()
    pl.when(m <= low)(lambda: signal(barrier, dp, jnp.minimum(m + 1, last)))
    pl.when(inner & (x == 0))(lambda: signal(barrier, beside, m))
    pl.when(inner & (y == 0))(lambda: signal(barrier, above, m))
    pl.when(inner & (c == 1))(lambda: signal(barrier, partner, m))
    load_spare.start()
    load_own.start()
    load_text.start()
    greeters = (m > 0).astype(jnp.int32) + jnp.where(inner, x + y + 1 - c, 0)
    pl.when(greeters > 0)(lambda: pl.semaphore_wait(barrier, greeters))
    pl.when(m == low + 1)(lambda: signal(barrier, dp, last))
    pl.when((m > 0) & inner)(lambda: signal(word.at[ACROSS_Z], dp, jnp.maximum(m - 1, 0)))
    pl.when(inner & (x == 1))(lambda: signal(word.at[ACROSS_X], beside, m))
    pl.when(inner & (y == 1))(lambda: signal(word.at[ACROSS_Y], above, m))
    pl.when(inner & (c == 0))(lambda: signal(word.at[ACROSS_CORE], partner, m))

    def hear(cond, which):
        pl.when(cond)(lambda: pl.semaphore_wait(word.at[which], 1))

    @pl.when(jnp.logical_not(inner))
    def _():
        hear(m == 0, ACROSS_Z)
        load_spare.wait()

        def halves_far():
            send(spare.at[1 - a], img.at[FAR, 0], spare_send, img_recv.at[FAR, 0], dp, far)

        def halves_near():
            send(spare.at[a], img.at[NEAR, 0], spare_send, img_recv.at[NEAR, 0], dp, near)

        pl.when(m != 0)(halves_far)
        halves_near()

        @pl.when(m == 0)
        def _():
            pl.semaphore_wait(word.at[BEYOND], 1)
            halves_far()

        load_text.wait()
        for q in range(CHUNKS):
            send(
                txt.at[OWN, 0, q], txt.at[NEAR, 0, q], text_send, txt_recv.at[NEAR, q], dp, near
            )
        load_own.wait()
        landed(spare, spare_send)
        landed(txt.at[OWN, 0], text_send)

    @pl.when(inner)
    def _():
        @pl.when(m == low)
        def _():
            pl.semaphore_wait(word.at[ACROSS_Z], 1)
            signal(word.at[BEYOND], dp, 0)

        load_spare.wait()
        send(spare.at[1 - a], img.at[OTHER, 0], spare_send, img_recv.at[OTHER, 0], dp, other)
        load_text.wait()
        for q in range(CHUNKS):
            send(
                txt.at[OWN, 0, q], txt.at[OTHER, 0, q], text_send, txt_recv.at[OTHER, q], dp, other
            )
        load_own.wait()

        def spread(p):
            send(img.at[p, 0], img.at[p, 1], xy_send, img_recv.at[p, 1], beside, m)
            send(img.at[p, 0], img.at[p, 2], xy_send, img_recv.at[p, 2], above, m)

        def relay(p):
            landed(img.at[p, 1 + c], img_recv.at[p, 1 + c])
            to = jnp.where(c == 0, above, beside)
            send(img.at[p, 1 + c], img.at[p, 3], xy_send, img_recv.at[p, 3], to, m)

        def texts_to_partner(p):
            send(txt.at[p, 0], txt.at[p, 1], pair_send, pair_recv.at[p], partner, m)

        def add(positions, first):
            lane_img, sub_img, lane_txt, sub_txt, rc, cr = ([] for _ in range(6))
            for p in positions:
                u = img[p].reshape(PLANE * half, img.shape[3])
                t = txt[p].reshape(CORES * rows, txt.shape[4])
                rc.append(dot_t(t, u))
                cr.append(dot_t(u, t))
                l, s = squares(u)
                lane_img.append(l)
                sub_img.append(s)
                l, s = squares(t)
                lane_txt.append(l)
                sub_txt.append(s)
            parts = []
            for ref, terms in (
                (by_row, rc),
                (by_col, cr),
                (img_lane, lane_img),
                (img_sub, sub_img),
                (txt_lane, lane_txt),
                (txt_sub, sub_txt),
            ):
                total = functools.reduce(lambda p, q: p + q, terms)
                parts.append(total if first else ref[...] + total)
            return parts

        hear(x == 0, ACROSS_X)
        hear(y == 0, ACROSS_Y)
        spread(OWN)
        hear(c == 1, ACROSS_CORE)
        texts_to_partner(OWN)

        relay(OWN)
        landed(img.at[OTHER, 0], img_recv.at[OTHER, 0])
        spread(OTHER)
        landed(img.at[NEAR, 0], img_recv.at[NEAR, 0])
        spread(NEAR)

        def forward(q):
            landed(txt.at[NEAR, 0, q], txt_recv.at[NEAR, q])
            send(txt.at[NEAR, 0, q], txt.at[FAR, 0, q], text_send, txt_recv.at[FAR, q], dp, other)

        forward(0)
        landed(img.at[OWN, 3], img_recv.at[OWN, 3])
        landed(img.at[FAR, 0], img_recv.at[FAR, 0])
        send(img.at[FAR, 0], img.at[FAR, 3], xy_send, img_recv.at[FAR, 3], across, m)
        spread(FAR)
        relay(OTHER)
        for q in range(1, CHUNKS):
            forward(q)
        texts_to_partner(NEAR)
        relay(NEAR)
        for q in range(CHUNKS):
            landed(txt.at[OTHER, 0, q], txt_recv.at[OTHER, q])
        texts_to_partner(OTHER)

        landed(img.at[OWN, 2 - c], img_recv.at[OWN, 2 - c])
        landed(txt.at[OWN, 1], pair_recv.at[OWN])
        for p in (OTHER, NEAR):
            landed(img.at[p, 2 - c], img_recv.at[p, 2 - c])
            landed(img.at[p, 3], img_recv.at[p, 3])
            landed(txt.at[p, 1], pair_recv.at[p])
        for ref, value in zip(
            (by_row, by_col, img_lane, img_sub, txt_lane, txt_sub),
            add((OWN, OTHER, NEAR), True),
        ):
            ref[...] = value

        for q in range(CHUNKS):
            landed(txt.at[FAR, 0, q], txt_recv.at[FAR, q])
        texts_to_partner(FAR)
        for k in range(1, PLANE):
            landed(img.at[FAR, k], img_recv.at[FAR, k])
        landed(txt.at[FAR, 1], pair_recv.at[FAR])

        rc, cr, lane_img, sub_img, lane_txt, sub_txt = add((FAR,), False)

        def inverse(total):
            return lax.rsqrt(total + 1e-06)

        scale = scale_ref[0]
        scores = rc * (scale * inverse(sub_txt)) * inverse(lane_img[0:1])
        row_top, row_total = top_total(scores)
        message = jnp.concatenate([row_top, row_total], axis=0)
        for k in range(PLANE):
            row_msg[k, :, 0:half] = message[:, k * half : (k + 1) * half]
        chips = (dp, beside, above, across)
        for z in range(DEPTH):
            for k in reversed(range(PLANE)):

                def row_to(k=k, z=z):
                    send(row_msg.at[k], row_got.at[a, k], row_send, row_recv, chips[k], z)

                if k:
                    row_to()
                else:
                    pl.when(m != z)(row_to)
        row_got[a, 0, :, 0:half] = message[:, 0:half]

        scores_own = scores[0:rows, 0:half]
        text_row = lax.broadcasted_iota(jnp.int32, scores_own.shape, 0) - a * half
        image_row = lax.broadcasted_iota(jnp.int32, scores_own.shape, 1)
        matched = jnp.sum(
            jnp.where(text_row == image_row, scores_own, 0.0), axis=0, keepdims=True
        )
        scores = cr * (scale * inverse(sub_img)) * inverse(lane_txt[0:1])
        message = jnp.concatenate(top_total(scores), axis=0)
        for k in range(CORES):
            col_msg[k, 0:2, 0:rows] = message[:, k * rows : (k + 1) * rows]
        col_msg[0, 2:3, 0:half] = matched
        for z in range(DEPTH):
            send(col_msg.at[1], col_got.at[a, 1], col_send, col_recv, partner, z)
            pl.when(m != z)(
                lambda: send(col_msg.at[0], col_got.at[a, 0], col_send, col_recv, dp, z)
            )
        col_got[a, 0, 0:2, 0:rows] = message[:, 0:rows]
        col_got[a, 0, 2:3, 0:half] = matched

        landed(img.at[0:3], xy_send)
        landed(img.at[0:2], pair_send)
        landed(img.at[0], text_send)
        landed(img.at[0, 0], spare_send)

    pl.when(inner)(lambda: landed(row_tally.at[0 : 2 * PLANE - 1], row_recv))
    pl.when(jnp.logical_not(inner))(lambda: landed(row_tally.at[0 : 2 * PLANE], row_recv))
    row_lse = []
    for w in range(2):
        tops = row_got[w, :, 0, 0:half]
        totals = row_got[w, :, 1, 0:half]
        peak = jnp.max(tops, axis=0, keepdims=True)
        row_lse.append(
            peak + jnp.log(jnp.sum(totals * jnp.exp(tops - peak), axis=0, keepdims=True))
        )
    pl.when(inner)(lambda: landed(col_tally.at[0:3], col_recv))
    pl.when(jnp.logical_not(inner))(lambda: landed(col_tally.at[0:4], col_recv))
    got = col_got[...].reshape(2 * CORES, *col_got.shape[2:])
    tops = got[:, 0, 0:rows]
    totals = got[:, 1, 0:rows]
    peak = jnp.max(tops, axis=0, keepdims=True)
    col_lse = peak + jnp.log(jnp.sum(totals * jnp.exp(tops - peak), axis=0, keepdims=True))
    matched = jnp.concatenate([col_got[w, 0, 2:3, 0:half] for w in range(2)], axis=1)
    out_ref[...] = jnp.concatenate([jnp.concatenate(row_lse, axis=1), col_lse], axis=0) - matched

    @pl.when(inner)
    def _():
        landed(row_tally.at[0 : DEPTH * PLANE - 1], row_send)
        landed(col_tally.at[0 : DEPTH * CORES - 1], col_send)


def kernel_on_device(images, texts, logit_scale):
    rows, width = images.shape
    half = rows // 2
    lanes = 128 * pl.cdiv(rows, 128)
    half_lanes = 128 * pl.cdiv(half, 128)
    wide_img = PLANE * half
    wide_txt = CORES * rows
    dma = pltpu.SemaphoreType.DMA
    vmem = pl.BlockSpec(memory_space=pltpu.VMEM)
    hbm = pl.BlockSpec(memory_space=pl.ANY)
    losses = pl.pallas_call(
        loss_kernel,
        out_shape=pltpu.VMEM((2, rows), F32),
        in_specs=[pl.BlockSpec(memory_space=pltpu.SMEM), hbm, hbm],
        out_specs=vmem,
        scratch_shapes=[
            pltpu.VMEM((DEPTH, PLANE, half, width), images.dtype),
            pltpu.VMEM((2, half, width), images.dtype),
            pltpu.VMEM((DEPTH, CORES, CHUNKS, rows // CHUNKS, width), texts.dtype),
            pltpu.VMEM((wide_txt, wide_img), F32),
            pltpu.VMEM((wide_img, wide_txt), F32),
            pltpu.VMEM((8, wide_img), F32),
            pltpu.VMEM((8, wide_txt), F32),
            pltpu.VMEM((wide_img, 1), F32),
            pltpu.VMEM((wide_txt, 1), F32),
            pltpu.VMEM((PLANE, 2, half_lanes), F32),
            pltpu.VMEM((CORES, 4, lanes), F32),
            pltpu.VMEM((2, PLANE, 2, half_lanes), F32),
            pltpu.VMEM((2, CORES, 4, lanes), F32),
            pltpu.VMEM((DEPTH * PLANE, 2, half_lanes), F32),
            pltpu.VMEM((DEPTH * CORES, 4, lanes), F32),
            dma((3,)),
            dma((DEPTH, PLANE)),
            dma((DEPTH, CHUNKS)),
            dma((DEPTH,)),
            dma(()),
            dma(()),
            pltpu.SemaphoreType.REGULAR((5,)),
            dma(()),
            dma(()),
            dma(()),
            dma(()),
            dma(()),
            dma(()),
        ],
        compiler_params=pltpu.CompilerParams(collective_id=0, has_side_effects=True),
    )(
        logit_scale,
        images.reshape(2, half, width),
        texts.reshape(CHUNKS, rows // CHUNKS, width),
    )
    return losses[0], losses[1]


def normalize(rows):
    values = rows.astype(F32)
    return (values * lax.rsqrt(jnp.sum(values * values, axis=1, keepdims=True) + 1e-06)).astype(
        jnp.bfloat16
    )


def collectives_on_device(images, texts, logit_scale):
    count = lax.axis_size("dp")
    m = lax.axis_index("mp")
    image_unit = normalize(lax.all_gather(images, "mp", axis=1, tiled=True))
    text_unit = normalize(lax.all_to_all(texts, "mp", split_axis=0, concat_axis=1, tiled=True))
    scale = logit_scale[0]
    quarter = text_unit.shape[0]
    mine = lax.dynamic_slice_in_dim(image_unit, m * quarter, quarter, 0)
    matched = scale * jnp.sum(mine.astype(F32) * text_unit.astype(F32), axis=1)
    scores = scale * dot_t(lax.all_gather(text_unit, "dp", axis=0, tiled=True), image_unit)
    row_top = jnp.max(scores, axis=0)
    row_total = jnp.sum(jnp.exp(scores - row_top[None, :]), axis=0)
    col_top = jnp.max(scores, axis=1)
    col_total = jnp.sum(jnp.exp(scores - col_top[:, None]), axis=1)
    got_top, got_total = (
        lax.all_to_all(v.reshape(count, quarter), "dp", split_axis=0, concat_axis=0, tiled=True)
        for v in (col_top, col_total)
    )
    col_peak = jnp.max(got_top, axis=0)
    col_lse = col_peak + jnp.log(jnp.sum(got_total * jnp.exp(got_top - col_peak[None, :]), axis=0))
    row_peak = lax.pmax(row_top, "mp")
    row_lse = row_peak + jnp.log(lax.psum(row_total * jnp.exp(row_top - row_peak), "mp"))
    col_full = lax.all_gather(col_lse, "mp", axis=0, tiled=True)
    matched_full = lax.all_gather(matched, "mp", axis=0, tiled=True)
    return row_lse - matched_full, col_full - matched_full


def solution(mesh):
    dp, mp = mesh.shape["dp"], mesh.shape["mp"]
    small = dp == CORES * PLANE and mp == DEPTH
    body = kernel_on_device if small else collectives_on_device
    return jax.shard_map(
        body,
        mesh=mesh,
        in_specs=(P("dp", "mp"), P("dp", "mp"), P()),
        out_specs=(P("dp"), P("dp")),
        check_vma=False,
    )
```

time: 24.7 us -> 25.2 us (1.020)
  Pallas kernels: 22.6 us -> 23.2 us
    pallas_call x1, Pallas kernels: 22.6 us -> 23.2 us  [kernel_on_device(): pl.pallas_call(loss_kernel, out_shape=pltpu.VMEM((2, rows), F32), in_spec...]
where the time goes in v2:
time: 25.2 us; the launch traced here: 25.1 us
  Pallas kernels  23.2 us (92%)
  between operations  1.28 us (5%)
  local copies, waits for them, and re-layouts  0.57 us (2%)
    pallas_call x1, Pallas kernels, kernel_on_device(): pl.pallas_call(loss_kernel, out_shape=pltpu.VMEM((2, rows), F32), in_spec...  23.2 us
    slice x1, local copies, waits for them, and re-layouts, kernel_on_device(): return (losses[0], losses[1])  0.57 us

profile of v2, /device:TPU:0, one launch (start us, length us, event | category | flops | bytes accessed | tf_op | source)
XLA Modules:
  0.0 25.1 jit_solution(6346992313780168691)
XLA Ops:
  1.3 23.2 %shard_map.50 = f32[2,192]{1,0:T(2,128)S(1)} custom-call(f32[1]{0:T(128)S(6)} %copy.5.scale_ref, bf16[2,96,256]{2,1,0:T(8,128)(2,1)} %bitcast.4, bf16[2,96,256]{2,1,0:T(8,128)(2,1)} %bitcast.5), custom_call_target="tpu_custom_call" | custom-call | tf_op jit(solution)/shard_map/pallas_call | solution.py:349
  24.5 0.6 %fusion = (f32[1,192]{1,0:T(1,128)}, f32[1,192]{1,0:T(1,128)}) fusion(f32[2,192]{1,0:T(2,128)S(1)} %shard_map.50), kind=kLoop, calls=%fused_computation | loop fusion | bytes 3072 | tf_op jit(solution)/shard_map/slice | solution.py:390

commit v3 on v2

--- a/solution.py
+++ b/solution.py
@@ -161,6 +161,22 @@
 
     @pl.when(inner)
     def _():
+        def texts_to_partner(p):
+            send(txt.at[p, 0], txt.at[p, 1], pair_send, pair_recv.at[p], partner, m)
+
+        def cross(p):
+            send(img.at[p, 0], img.at[p, 3], xy_send, img_recv.at[p, 3], across, m)
+
+        def spread(p):
+            send(img.at[p, 0], img.at[p, 1], xy_send, img_recv.at[p, 1], beside, m)
+            send(img.at[p, 0], img.at[p, 2], xy_send, img_recv.at[p, 2], above, m)
+
+        load_own.wait()
+        hear(x == 0, ACROSS_X)
+        hear(y == 0, ACROSS_Y)
+        signal(word.at[BEYOND], beside, m)
+        spread(OWN)
+
         @pl.when(m == low)
         def _():
             pl.semaphore_wait(word.at[ACROSS_Z], 1)
@@ -173,96 +189,58 @@
             send(
                 txt.at[OWN, 0, q], txt.at[OTHER, 0, q], text_send, txt_recv.at[OTHER, q], dp, other
             )
-        load_own.wait()
-
-        def spread(p):
-            send(img.at[p, 0], img.at[p, 1], xy_send, img_recv.at[p, 1], beside, m)
-            send(img.at[p, 0], img.at[p, 2], xy_send, img_recv.at[p, 2], above, m)
-
-        def relay(p):
-            landed(img.at[p, 1 + c], img_recv.at[p, 1 + c])
-            to = jnp.where(c == 0, above, beside)
-            send(img.at[p, 1 + c], img.at[p, 3], xy_send, img_recv.at[p, 3], to, m)
-
-        def texts_to_partner(p):
-            send(txt.at[p, 0], txt.at[p, 1], pair_send, pair_recv.at[p], partner, m)
-
-        def add(positions, first):
-            lane_img, sub_img, lane_txt, sub_txt, rc, cr = ([] for _ in range(6))
-            for p in positions:
-                u = img[p].reshape(PLANE * half, img.shape[3])
-                t = txt[p].reshape(CORES * rows, txt.shape[4])
-                rc.append(dot_t(t, u))
-                cr.append(dot_t(u, t))
-                l, s = squares(u)
-                lane_img.append(l)
-                sub_img.append(s)
-                l, s = squares(t)
-                lane_txt.append(l)
-                sub_txt.append(s)
-            parts = []
-            for ref, terms in (
-                (by_row, rc),
-                (by_col, cr),
-                (img_lane, lane_img),
-                (img_sub, sub_img),
-                (txt_lane, lane_txt),
-                (txt_sub, sub_txt),
-            ):
-                total = functools.reduce(lambda p, q: p + q, terms)
-                parts.append(total if first else ref[...] + total)
-            return parts
-
-        hear(x == 0, ACROSS_X)
-        hear(y == 0, ACROSS_Y)
-        spread(OWN)
+        pl.semaphore_wait(word.at[BEYOND], 1)
+        cross(OWN)
         hear(c == 1, ACROSS_CORE)
         texts_to_partner(OWN)
 
-        relay(OWN)
-        landed(img.at[OTHER, 0], img_recv.at[OTHER, 0])
-        spread(OTHER)
-        landed(img.at[NEAR, 0], img_recv.at[NEAR, 0])
-        spread(NEAR)
+        def pass_on(p):
+            landed(img.at[p, 0], img_recv.at[p, 0])
+            cross(p)
+            spread(p)
 
         def forward(q):
             landed(txt.at[NEAR, 0, q], txt_recv.at[NEAR, q])
             send(txt.at[NEAR, 0, q], txt.at[FAR, 0, q], text_send, txt_recv.at[FAR, q], dp, other)
 
+        def complete(p):
+            for k in range(1, PLANE):
+                landed(img.at[p, k], img_recv.at[p, k])
+            landed(txt.at[p, 1], pair_recv.at[p])
+
+        def terms(p):
+            u = img[p].reshape(PLANE * half, img.shape[3])
+            t = txt[p].reshape(CORES * rows, txt.shape[4])
+            return (dot_t(t, u), dot_t(u, t)) + squares(u) + squares(t)
+
+        totals = (by_row, by_col, img_lane, img_sub, txt_lane, txt_sub)
+
+        pass_on(OTHER)
+        pass_on(NEAR)
         forward(0)
-        landed(img.at[OWN, 3], img_recv.at[OWN, 3])
-        landed(img.at[FAR, 0], img_recv.at[FAR, 0])
-        send(img.at[FAR, 0], img.at[FAR, 3], xy_send, img_recv.at[FAR, 3], across, m)
-        spread(FAR)
-        relay(OTHER)
+        pass_on(FAR)
         for q in range(1, CHUNKS):
             forward(q)
         texts_to_partner(NEAR)
-        relay(NEAR)
         for q in range(CHUNKS):
             landed(txt.at[OTHER, 0, q], txt_recv.at[OTHER, q])
         texts_to_partner(OTHER)
 
-        landed(img.at[OWN, 2 - c], img_recv.at[OWN, 2 - c])
-        landed(txt.at[OWN, 1], pair_recv.at[OWN])
+        complete(OWN)
+        for ref, term in zip(totals, terms(OWN)):
+            ref[...] = term
         for p in (OTHER, NEAR):
-            landed(img.at[p, 2 - c], img_recv.at[p, 2 - c])
-            landed(img.at[p, 3], img_recv.at[p, 3])
-            landed(txt.at[p, 1], pair_recv.at[p])
-        for ref, value in zip(
-            (by_row, by_col, img_lane, img_sub, txt_lane, txt_sub),
-            add((OWN, OTHER, NEAR), True),
-        ):
-            ref[...] = value
+            complete(p)
+            for ref, term in zip(totals, terms(p)):
+                ref[...] += term
 
         for q in range(CHUNKS):
             landed(txt.at[FAR, 0, q], txt_recv.at[FAR, q])
         texts_to_partner(FAR)
-        for k in range(1, PLANE):
-            landed(img.at[FAR, k], img_recv.at[FAR, k])
-        landed(txt.at[FAR, 1], pair_recv.at[FAR])
-
-        rc, cr, lane_img, sub_img, lane_txt, sub_txt = add((FAR,), False)
+        complete(FAR)
+        rc, cr, lane_img, sub_img, lane_txt, sub_txt = (
+            ref[...] + term for ref, term in zip(totals, terms(FAR))
+        )
 
         def inverse(total):
             return lax.rsqrt(total + 1e-06)

time: 25.2 us -> 22.6 us (0.90)
  Pallas kernels: 23.2 us -> 20.6 us
    pallas_call x1, Pallas kernels: 23.2 us -> 20.6 us  [kernel_on_device(): pl.pallas_call(loss_kernel, out_shape=pltpu.VMEM((2, rows), F32), in_spec...]
where the time goes in v3:
time: 22.6 us; the launch traced here: 22.5 us
  Pallas kernels  20.6 us (91%)
  between operations  1.28 us (6%)
  local copies, waits for them, and re-layouts  0.57 us (3%)
    pallas_call x1, Pallas kernels, kernel_on_device(): pl.pallas_call(loss_kernel, out_shape=pltpu.VMEM((2, rows), F32), in_spec...  20.6 us
    slice x1, local copies, waits for them, and re-layouts, kernel_on_device(): return (losses[0], losses[1])  0.57 us

profile of v3, /device:TPU:0, one launch (start us, length us, event | category | flops | bytes accessed | tf_op | source)
XLA Modules:
  0.0 22.5 jit_solution(14666955883436784511)
XLA Ops:
  1.3 20.6 %shard_map.50 = f32[2,192]{1,0:T(2,128)S(1)} custom-call(f32[1]{0:T(128)S(6)} %copy.5.scale_ref, bf16[2,96,256]{2,1,0:T(8,128)(2,1)} %bitcast.4, bf16[2,96,256]{2,1,0:T(8,128)(2,1)} %bitcast.5), custom_call_target="tpu_custom_call" | custom-call | tf_op jit(solution)/shard_map/pallas_call | solution.py:327
  21.9 0.6 %fusion = (f32[1,192]{1,0:T(1,128)}, f32[1,192]{1,0:T(1,128)}) fusion(f32[2,192]{1,0:T(2,128)S(1)} %shard_map.50), kind=kLoop, calls=%fused_computation | loop fusion | bytes 3072 | tf_op jit(solution)/shard_map/slice | solution.py:368
